TPU v7x, 256 devices: a whole 4x4x8 slice. The times are simulated.
256 devices in a mesh: seq: 32 (over y, z), tp: 8 (over x, core).
Axes of the slice: x: 4, y: 4, z: 8, core: 2. Of those that a mesh axis runs over, the one named last changes fastest.
Arguments:
- tokens: bfloat16 [24576, 2048], P('seq', 'tp'), may hold values from -20 to 20
- w_query: bfloat16 [2048, 2048], P(None, 'tp'), may hold values from -0.125 to 0.125
- w_key: bfloat16 [2048, 2048], P(None, 'tp'), may hold values from -0.125 to 0.125
- w_value: bfloat16 [2048, 2048], P(None, 'tp'), may hold values from -0.125 to 0.125
- head_gain: float32 [2048], P('tp'), may hold values from 0.5 to 1.5
- w_out: bfloat16 [2048, 2048], P('tp'), may hold values from -0.125 to 0.125
- norm_gain: float32 [2048], replicated, may hold values from 0.5 to 1.5
- w_gate: bfloat16 [2048, 8192], P('seq', 'tp'), may hold values from -0.125 to 0.125
- w_up: bfloat16 [2048, 8192], P('seq', 'tp'), may hold values from -0.125 to 0.125
- w_down: bfloat16 [8192, 2048], P('tp', 'seq'), may hold values from -0.0625 to 0.0625
Outputs:
- layer_out: bfloat16 [24576, 2048], P('seq', 'tp')
All inputs are finite; a program needn't handle non-finite values.
Results may differ from a plain program's by a relative error of at most 0.009.
Values may be sent and summed in bfloat16 or wider, within the bound.
No kernel may reach another device: no remote copies, remote signals or barrier semaphores. Data moves between devices by JAX's collectives and lax.ppermute only.
A program may use at most 128 MiB of HBM per device.

v0:
```python
import jax
import jax.numpy as jnp
from jax import lax
from jax.sharding import Mesh
from jax.sharding import PartitionSpec as P

HD = 128
SEQ = ("seq_0", "seq_1")


def nothing_yet(array, identity):
    return jnp.zeros_like(array) + jnp.asarray(identity, array.dtype)


def entering(array, axes, combine, identity):
    before = start = nothing_yet(array, identity)
    total = array
    for axis in reversed(axes):
        peers, position = (lax.axis_size(axis), lax.axis_index(axis))
        pieces = lax.all_gather(total.astype(jnp.bfloat16), axis)
        inside, total = (start, start)
        for k in range(peers):
            passed = k < position
            total = combine(total, pieces[k].astype(array.dtype))
            inside = jnp.where(passed, total, inside)
        before = combine(inside, before)
    return before


def in_one_piece(arrays, axis, dim, along):
    ends, at = ([], 0)
    for a in arrays[:-1]:
        at += a.shape[along]
        ends.append(at)
    both = jnp.concatenate(arrays, axis=along)
    return tuple(jnp.split(lax.all_gather(both, axis, axis=dim, tiled=True), ends, axis=along))


def split_up(array, dim, peers):
    shape = array.shape
    tiles = array.reshape(*shape[:dim], peers, shape[dim] // peers, *shape[dim + 1 :])
    return jnp.moveaxis(tiles, dim, 0)


def sum_at_owner(array, axis, dim):
    tiles = split_up(array, dim, lax.axis_size(axis))
    arrived = lax.all_to_all(tiles, axis, split_axis=0, concat_axis=0, tiled=True)
    return arrived.astype(jnp.float32).sum(axis=0)


def add_states(earlier, later):
    return earlier + later


def body(tokens, w_query, w_key, w_value, head_gain, w_out, norm_gain, w_gate, w_up, w_down):
    length = tokens.shape[0]
    width_here = tokens.shape[1]
    heads_here = w_query.shape[1] // HD
    features = lax.all_gather(tokens, "tp", axis=1, tiled=True)

    def project(weight):
        product = jnp.dot(features, weight, preferred_element_type=jnp.float32)
        return product.astype(jnp.bfloat16).reshape(length, heads_here, HD)

    query = project(w_query)
    keys_local = project(w_key)
    values_local = project(w_value)
    scores = jnp.einsum("ihd,jhd->hij", query, keys_local, preferred_element_type=jnp.float32)
    causal = jnp.arange(length)[:, None] >= jnp.arange(length)[None, :]
    scores = jnp.where(causal[None], scores, 0.0).astype(jnp.bfloat16)
    inside = jnp.einsum("hij,jhd->ihd", scores, values_local, preferred_element_type=jnp.float32)
    own_state = jnp.einsum(
        "jhd,jhe->hde", keys_local, values_local, preferred_element_type=jnp.float32
    )
    history = entering(own_state, SEQ, add_states, jnp.zeros_like(own_state))
    carried = jnp.einsum(
        "ihd,hde->ihe", query, history.astype(jnp.bfloat16), preferred_element_type=jnp.float32
    )
    mixed = inside + carried
    scale = lax.rsqrt(jnp.mean(mixed * mixed, axis=-1, keepdims=True) + 1e-06)
    normed = (mixed * scale * head_gain.reshape(heads_here, HD)).astype(jnp.bfloat16)
    normed = normed.reshape(length, heads_here * HD)
    partial_value = jnp.dot(normed, w_out, preferred_element_type=jnp.float32)
    own_column = lax.axis_index("tp") * width_here
    summed = lax.psum(partial_value.astype(jnp.bfloat16), "tp").astype(jnp.float32)
    resid_whole = features.astype(jnp.float32) + summed
    factor = lax.rsqrt(jnp.mean(resid_whole * resid_whole, axis=-1, keepdims=True) + 1e-05)
    ffn_in = (resid_whole * factor * norm_gain).astype(jnp.bfloat16)
    resid = lax.dynamic_slice_in_dim(resid_whole, own_column, width_here, 1)
    pieces = in_one_piece((w_gate, w_up), SEQ, 0, 1)
    gate_sum = jnp.dot(ffn_in, pieces[0], preferred_element_type=jnp.float32)
    upward_sum = jnp.dot(ffn_in, pieces[1], preferred_element_type=jnp.float32)
    hidden = (jax.nn.silu(gate_sum) * upward_sum).astype(jnp.bfloat16)
    terms = jnp.dot(
        hidden, lax.all_gather(w_down, SEQ, axis=1, tiled=True), preferred_element_type=jnp.float32
    )
    mlp_share = sum_at_owner(terms.astype(jnp.bfloat16), "tp", 1)
    return (resid + mlp_share).astype(jnp.bfloat16)


def solution(mesh):
    finer = Mesh(mesh.devices.reshape(4, 8, mesh.shape["tp"]), ("seq_0", "seq_1", "tp"))
    return jax.shard_map(
        body,
        mesh=finer,
        in_specs=(
            P(SEQ, "tp"),
            P(None, "tp"),
            P(None, "tp"),
            P(None, "tp"),
            P("tp"),
            P("tp", None),
            P(),
            P(SEQ, "tp"),
            P(SEQ, "tp"),
            P("tp", SEQ),
        ),
        out_specs=P(SEQ, "tp"),
        check_vma=False,
    )
```

profile of v0, /device:TPU:1, one launch (start us, length us, event | category | flops | bytes accessed | tf_op | source)
XLA Modules:
  0.0 356.1 jit_solution(3774338087254047791)
XLA Ops:
  7.4 0.0 copy-start
  7.4 0.0 all-gather.5.cloned.1.call-start
  7.4 0.7 all-gather.5.cloned.1.call-update
  8.1 0.0 all-reduce.2.cloned.1.call-start
  8.2 0.2 iota_compare_fusion
  8.3 39.5 %all-gather.5.cloned.1.call-done = bf16[768,2048]{1,0:T(8,128)(2,1)} async-done(((bf16[768,256]{1,0:T(8,128)(2,1)}), bf16[768,2048]{1,0:T(8,128)(2,1)}) %all-gather.5.cloned.1.call-update) | async-done | bytes 3145744 | tf_op jit(solution)/shard_map/all_gather | solution.py:59
  47.9 0.0 copy-start.1
  47.9 3.3 convolution_convert_fusion.2
  51.2 0.0 copy-done.1
  51.2 0.0 copy-start.5
  51.2 2.4 convolution_convert_fusion.4
  53.6 0.3 convolution_convert_fusion.5
  53.9 20.8 %all-gather = bf16[16,128,128]{2,1,0:T(8,128)(2,1)S(1)} all-gather(bf16[2,128,128]{2,1,0:T(8,128)(2,1)S(1)} %convolution_convert_fusion.5), channel_id=2, replica_groups=mesh['seq_0'=4,'seq_1'=8,'tp'=8] {'seq_1'}, dimensions={0}, use_global_device_ids=true | all-gather | bytes 589824 | tf_op jit(solution)/shard_map/all_gather | solution.py:20
  74.7 0.1 fusion.28
  74.7 9.7 %all_gather.22 = bf16[4,2,128,128]{3,2,1,0:T(8,128)(2,1)S(1)} all-gather(bf16[1,2,128,128]{3,2,1,0:T(8,128)(2,1)S(1)} %fusion.28), channel_id=1, replica_groups=mesh['seq_0'=4,'seq_1'=8,'tp'=8] {'seq_0'}, dimensions={0}, use_global_device_ids=true | all-gather | bytes 327680 | tf_op jit(solution)/shard_map/all_gather | solution.py:20
  84.5 0.0 copy-done.5
  84.5 1.1 convolution_convert_fusion.3
  85.6 0.0 copy-start.7
  85.6 0.7 copy-done.7
  86.3 1.3 fusion.29
  87.6 0.0 copy-start.4
  87.6 2.9 multiply_reduce_fusion.1
  90.5 0.0 copy-done.4
  90.5 0.1 multiply_convert_fusion.2
  90.6 0.0 copy-done
  90.6 2.7 convolution_convert_fusion.1
  93.4 0.0 copy-start.2
  93.4 0.0 copy-start.3
  93.4 0.0 all-reduce.2.cloned.1.call-update
  93.4 0.0 all-gather.7.cloned.1.call-start
  93.5 0.8 copy-done.2
  94.3 0.1 copy-done.3
  94.3 0.7 pad_maximum_fusion
  95.1 0.0 all-gather.7.cloned.1.call-update
  95.1 0.2 all-gather.9.cloned.1.call-start
  95.3 0.4 all-gather.9.cloned.1.call-update
  95.7 0.0 copy-start.6
  95.7 79.1 %all-reduce.2.cloned.1.call-done = bf16[768,2048]{1,0:T(8,128)(2,1)} async-done(((bf16[768,2048]{1,0:T(8,128)(2,1)}), bf16[768,2048]{1,0:T(8,128)(2,1)}) %all-reduce.2.cloned.1.call-update) | async-done | bytes 3145744 | tf_op jit(solution)/shard_map/psum | solution.py:85
  174.8 6.7 %convert_add_fusion = (f32[768,2048]{1,0:T(8,128)}, f32[768]{0:T(1024)S(1)}) fusion(bf16[768,2048]{1,0:T(8,128)(2,1)} %all-reduce.2.cloned.1.call-done, bf16[768,2048]{1,0:T(8,128)(2,1)} %all-gather.5.cloned.1.call-done), kind=kLoop, calls=%fused_computation.3 | loop fusion | flops 7863552 | bytes 12585984 | tf_op jit(solution)/shard_map/add | solution.py:86
  181.6 19.3 %all-gather.7.cloned.1.call-done = bf16[2048,2048]{1,0:T(8,128)(2,1)} async-done(((bf16[64,2048]{1,0:T(8,128)(2,1)}), bf16[2048,2048]{1,0:T(8,128)(2,1)}) %all-gather.7.cloned.1.call-update) | async-done | bytes 8388624 | tf_op jit(solution)/shard_map/all_gather | solution.py:36
  200.9 0.0 copy-done.6
  200.9 9.2 %fusion = f32[768,1024]{1,0:T(8,128)} fusion(bf16[2048,2048]{1,0:T(8,128)(2,1)} %all-gather.7.cloned.1.call-done, f32[2048]{0:T(1024)S(1)} %copy-done.6, f32[768]{0:T(1024)S(1)} %add_rsqrt_fusion.1, bf16[768,2048]{1,0:T(8,128)(2,1)} %all-reduce.2.cloned.1.call-done, bf16[768,2048]{1,0:T(8,128)(2,1)} %all-gather.5.cloned.1.call-done), kind=kOutput, calls=%fused_computation.5 | convolution fusion | flops 3230662656 | bytes 13642752 | tf_op jit(solution)/shard_map/dot_general | solution.py:92
  210.2 69.3 %all-gather.9.cloned.1.call-done = bf16[1024,2048]{0,1:T(8,128)(2,1)} async-done(((bf16[1024,64]{0,1:T(8,128)(2,1)}), bf16[1024,2048]{0,1:T(8,128)(2,1)}) %all-gather.9.cloned.1.call-update) | async-done | bytes 4194320 | tf_op jit(solution)/shard_map/all_gather | solution.py:95
  279.5 14.9 %convolution_convert_fusion = bf16[768,2048]{1,0:T(8,128)(2,1)} fusion(bf16[1024,2048]{0,1:T(8,128)(2,1)} %all-gather.9.cloned.1.call-done, f32[768,1024]{1,0:T(8,128)} %fusion, bf16[2048,2048]{1,0:T(8,128)(2,1)} %all-gather.7.cloned.1.call-done, f32[2048]{0:T(1024)S(1)} %copy-done.6, f32[768]{0:T(1024)S(1)} %add_rsqrt_fusion.1, ...), kind=kOutput, calls=%fused_computation.9 | convolution fusion | flops 6458179584 | bytes 20982784 | tf_op jit(solution)/shard_map/dot_general | solution.py:94
  294.4 3.7 %copy.23 = bf16[96,8,8,256]{3,2,0,1:T(8,128)(2,1)} copy(bf16[96,8,8,256]{3,2,1,0:T(8,128)(2,1)} %bitcast.58) | data formatting | bytes 6291456 | tf_op jit(solution)/shard_map/reshape | solution.py:41
  298.1 8.6 %all-to-all-start = ((bf16[8,768,256]{2,1,0:T(8,128)(2,1)}), bf16[8,768,256]{2,1,0:T(8,128)(2,1)}, u32[]{:S(2)}, u32[]{:S(2)}) async-start(bf16[8,768,256]{2,1,0:T(8,128)(2,1)} %bitcast.57), calls=%async_computation | async-start | bytes 6291456 | tf_op jit(solution)/shard_map/all_to_all | solution.py:47
  306.7 37.6 %all-to-all-done = bf16[8,768,256]{2,1,0:T(8,128)(2,1)} async-done(((bf16[8,768,256]{2,1,0:T(8,128)(2,1)}), bf16[8,768,256]{2,1,0:T(8,128)(2,1)}, u32[]{:S(2)}, u32[]{:S(2)}) %all-to-all-start) | async-done | bytes 3145760 | tf_op jit(solution)/shard_map/all_to_all | solution.py:47
  344.3 2.4 convert_reduce_fusion
  346.7 2.0 add_convert_fusion
  (2 shorter events, 0.0 us)
Async XLA Ops:
  7.4 83.3 %copy-start = (bf16[256,2048]{1,0:T(8,128)(2,1)S(1)}, bf16[256,2048]{1,0:T(8,128)(2,1)}, u32[]{:S(2)}) copy-start(bf16[256,2048]{1,0:T(8,128)(2,1)} %param.15) | copy-start | bytes 3145732
  7.4 40.5 %all-gather.5.cloned.1.call-start = ((), (), s32[]{:S(2)}) async-start(), calls=%async_computation.1 | async-start | bytes 3538944 | tf_op jit(solution)/shard_map/all_gather | solution.py:59
  8.1 166.7 %all-reduce.2.cloned.1.call-start = ((), (), s32[]{:S(2)}) async-start(), calls=%async_computation.2 | async-start | bytes 6291456 | tf_op jit(solution)/shard_map/psum | solution.py:85
  47.9 3.4 copy-start.1
  51.2 33.2 %copy-start.5 = (bf16[2048,256]{1,0:T(8,128)(2,1)S(1)}, bf16[2048,256]{1,0:T(8,128)(2,1)}, u32[]{:S(2)}) copy-start(bf16[2048,256]{1,0:T(8,128)(2,1)} %param.11) | copy-start | bytes 3145732
  85.6 0.7 copy-start.7
  87.6 2.9 copy-start.4
  93.4 0.9 copy-start.2
  93.4 1.0 copy-start.3
  93.4 107.5 %all-gather.7.cloned.1.call-start = ((), (), s32[]{:S(2)}) async-start(), calls=%async_computation.3 | async-start | bytes 8650752 | tf_op jit(solution)/shard_map/all_gather | solution.py:36
  95.1 184.4 %all-gather.9.cloned.1.call-start = ((), (), s32[]{:S(2)}) async-start(), calls=%async_computation.4 | async-start | bytes 4325376 | tf_op jit(solution)/shard_map/all_gather | solution.py:95
  95.7 105.2 %copy-start.6 = (f32[2048]{0:T(1024)S(1)}, f32[2048]{0:T(1024)}, u32[]{:S(2)}) copy-start(f32[2048]{0:T(1024)} %param.16) | copy-start | bytes 24580
  298.1 46.2 %all-to-all-start = ((bf16[8,768,256]{2,1,0:T(8,128)(2,1)}), bf16[8,768,256]{2,1,0:T(8,128)(2,1)}, u32[]{:S(2)}, u32[]{:S(2)}) async-start(bf16[8,768,256]{2,1,0:T(8,128)(2,1)} %bitcast.57), calls=%async_computation | async-start | bytes 6291456 | tf_op jit(solution)/shard_map/all_to_all | solution.py:47
Sparse Core Ops, SparseCore 0:
  10.0 37.8 all-gather.4
  93.5 81.2 all-reduce.1
Sparse Core Ops, SparseCore 1:
  96.5 104.4 all-gather.6
  203.4 76.1 all-gather.8
where the time goes:
time: 356 us
  waiting for transfers between devices  246 us (69%)
  matrix products  38.1 us (11%)
  blocking collectives  30.5 us (9%)
  between operations  15 us (4%)
  other arithmetic  12.2 us (3%)
  starting transfers between devices  8.92 us (3%)
  local copies, waits for them, and re-layouts  5.37 us (2%)
    psum x1, waiting for transfers between devices, body(): lax.psum(partial_value.astype(jnp.bfloat16), 'tp').astype(jnp.float32)  79.1 us
    all_gather x1, waiting for transfers between devices, body(): lax.all_gather(w_down, SEQ, axis=1, tiled=True)  69.3 us
    all_gather x1, waiting for transfers between devices, body(): features = lax.all_gather(tokens, 'tp', axis=1, tiled=True)  39.5 us
    all_to_all x1, waiting for transfers between devices, sum_at_owner(): lax.all_to_all(tiles, axis, split_axis=0, concat_axis=0, tiled=True)  37.6 us
    all_gather x2, blocking collectives, entering(): pieces = lax.all_gather(total.astype(jnp.bfloat16), axis)  30.5 us
    all_gather x1, waiting for transfers between devices, in_one_piece(): lax.all_gather(both, axis, axis=dim, tiled=True)  19.3 us
    dot_general x1, matrix products, body(): jnp.dot(hidden, lax.all_gather(w_down, SEQ, axis=1, tiled=True), preferre...  14.9 us
    dot_general x1, matrix products, body(): upward_sum = jnp.dot(ffn_in, pieces[1], preferred_element_type=jnp.float32)  9.24 us
  transfers between devices with their start and end apart: 5, of which 5 were waited for; matrix products, arithmetic and copies ran while one was open for 5% of the time, Pallas kernels for 0%

commit v1 on v0

--- a/solution.py
+++ b/solution.py
@@ -92,7 +92,11 @@
     upward_sum = jnp.dot(ffn_in, pieces[1], preferred_element_type=jnp.float32)
     hidden = (jax.nn.silu(gate_sum) * upward_sum).astype(jnp.bfloat16)
     terms = jnp.dot(
-        hidden, lax.all_gather(w_down, SEQ, axis=1, tiled=True), preferred_element_type=jnp.float32
+        hidden,
+        jnp.concatenate(
+            lax.all_to_all(jnp.stack([w_down] * lax.axis_size(SEQ)), SEQ, 0, 0), axis=1
+        ),
+        preferred_element_type=jnp.float32,
     )
     mlp_share = sum_at_owner(terms.astype(jnp.bfloat16), "tp", 1)
     return (resid + mlp_share).astype(jnp.bfloat16)

time: 356 us -> 332 us (0.933)
  waiting for transfers between devices: 246 us -> 214 us
  starting transfers between devices: 8.92 us -> 13.2 us
    all_gather x1 -> x0, waiting for transfers between devices: 69.3 us -> none  [body(): lax.all_gather(w_down, SEQ, axis=1, tiled=True)]
    all_gather x1, waiting for transfers between devices: 19.3 us -> 67.8 us  [in_one_piece(): lax.all_gather(both, axis, axis=dim, tiled=True)]
    psum x1, waiting for transfers between devices: 79.1 us -> 68.9 us  [body(): lax.psum(partial_value.astype(jnp.bfloat16), 'tp').astype(jnp.float32)]
    all_to_all x0 -> x1, starting transfers between devices: none -> 8.33 us  [body(): lax.all_to_all(jnp.stack([w_down] * lax.axis_size(SEQ)), SEQ, 0, 0)]
    all_to_all x1, starting transfers between devices: 8.61 us -> 4.82 us  [sum_at_owner(): lax.all_to_all(tiles, axis, split_axis=0, concat_axis=0, tiled=True)]
  transfers between devices with their start and end apart: 5 -> 5, of which waited for: 5 -> 4; matrix products, arithmetic and copies ran while one was open for 5% -> 6% of each run, Pallas kernels for 0% -> 0%
where the time goes in v1:
time: 332 us; the launch traced here: 331 us
  waiting for transfers between devices  214 us (64%)
  matrix products  38 us (11%)
  blocking collectives  30.5 us (9%)
  between operations  15 us (5%)
  starting transfers between devices  13.2 us (4%)
  other arithmetic  12 us (4%)
  local copies, waits for them, and re-layouts  7.94 us (2%)
    psum x1, waiting for transfers between devices, body(): lax.psum(partial_value.astype(jnp.bfloat16), 'tp').astype(jnp.float32)  68.9 us
    all_gather x1, waiting for transfers between devices, in_one_piece(): lax.all_gather(both, axis, axis=dim, tiled=True)  67.8 us
    all_gather x1, waiting for transfers between devices, body(): features = lax.all_gather(tokens, 'tp', axis=1, tiled=True)  39.5 us
    all_to_all x1, waiting for transfers between devices, sum_at_owner(): lax.all_to_all(tiles, axis, split_axis=0, concat_axis=0, tiled=True)  37.6 us
    all_gather x2, blocking collectives, entering(): pieces = lax.all_gather(total.astype(jnp.bfloat16), axis)  30.5 us
    dot_general x1, matrix products, body(): jnp.dot(hidden, jnp.concatenate(lax.all_to_all(jnp.stack([w_down] * lax.a...  14.8 us
    dot_general x1, matrix products, body(): upward_sum = jnp.dot(ffn_in, pieces[1], preferred_element_type=jnp.float32)  9.17 us
    all_to_all x1, starting transfers between devices, body(): lax.all_to_all(jnp.stack([w_down] * lax.axis_size(SEQ)), SEQ, 0, 0)  8.33 us
  transfers between devices with their start and end apart: 5, of which 4 were waited for; matrix products, arithmetic and copies ran while one was open for 6% of the time, Pallas kernels for 0%

profile of v1, /device:TPU:1, one launch (start us, length us, event | category | flops | bytes accessed | tf_op | source)
XLA Modules:
  0.0 331.1 jit_solution(11919737368756402043)
XLA Ops:
  7.4 0.0 copy-start
  7.4 0.0 all-gather.4.cloned.1.call-start
  7.4 0.7 all-gather.4.cloned.1.call-update
  8.1 0.0 all-reduce.2.cloned.1.call-start
  8.2 0.2 iota_compare_fusion
  8.3 39.5 %all-gather.4.cloned.1.call-done = bf16[768,2048]{1,0:T(8,128)(2,1)} async-done(((bf16[768,256]{1,0:T(8,128)(2,1)}), bf16[768,2048]{1,0:T(8,128)(2,1)}) %all-gather.4.cloned.1.call-update) | async-done | bytes 3145744 | tf_op jit(solution)/shard_map/all_gather | solution.py:59
  47.9 0.0 copy-start.1
  47.9 3.3 %convolution_convert_fusion.2 = bf16[768,256]{0,1:T(8,128)(2,1)S(1)} fusion(bf16[768,2048]{1,0:T(8,128)(2,1)} %all-gather.4.cloned.1.call-done, bf16[2048,256]{1,0:T(8,128)(2,1)} %param.12), kind=kOutput, calls=%fused_computation.20 | convolution fusion | flops 805502976 | bytes 4587520 | tf_op jit(solution)/shard_map/dot_general | solution.py:62
  51.2 0.0 copy-done.1
  51.2 0.0 copy-start.6
  51.2 2.4 convolution_convert_fusion.4
  53.6 0.3 convolution_convert_fusion.5
  53.9 20.8 %all-gather = bf16[16,128,128]{2,1,0:T(8,128)(2,1)S(1)} all-gather(bf16[2,128,128]{2,1,0:T(8,128)(2,1)S(1)} %convolution_convert_fusion.5), channel_id=2, replica_groups=mesh['seq_0'=4,'seq_1'=8,'tp'=8] {'seq_1'}, dimensions={0}, use_global_device_ids=true | all-gather | bytes 589824 | tf_op jit(solution)/shard_map/all_gather | solution.py:20
  74.7 0.1 fusion.28
  74.7 9.7 %all_gather.19 = bf16[4,2,128,128]{3,2,1,0:T(8,128)(2,1)S(1)} all-gather(bf16[1,2,128,128]{3,2,1,0:T(8,128)(2,1)S(1)} %fusion.28), channel_id=1, replica_groups=mesh['seq_0'=4,'seq_1'=8,'tp'=8] {'seq_0'}, dimensions={0}, use_global_device_ids=true | all-gather | bytes 327680 | tf_op jit(solution)/shard_map/all_gather | solution.py:20
  84.5 0.0 copy-done.6
  84.5 1.1 convolution_convert_fusion.3
  85.6 0.0 copy-start.8
  85.6 0.7 copy-done.8
  86.3 1.3 fusion.29
  87.6 0.0 copy-start.5
  87.6 2.9 multiply_reduce_fusion.1
  90.5 0.0 copy-done.5
  90.5 0.1 multiply_convert_fusion.2
  90.6 0.0 copy-done
  90.6 2.7 convolution_convert_fusion.1
  93.4 0.0 copy-start.3
  93.4 0.0 copy-start.4
  93.4 0.0 copy-start.2
  93.4 0.0 all-reduce.2.cloned.1.call-update
  93.4 0.0 all-gather.6.cloned.1.call-start
  93.5 0.8 copy-done.3
  94.3 0.1 copy-done.4
  94.3 0.7 pad_maximum_fusion
  95.1 0.0 all-gather.6.cloned.1.call-update
  95.1 0.0 copy-done.2
  95.1 2.6 stack.2
  97.7 8.3 %all-to-all-start = ((bf16[32,1024,64]{1,2,0:T(8,128)(2,1)}), bf16[32,1024,64]{1,2,0:T(8,128)(2,1)}, u32[]{:S(2)}, u32[]{:S(2)}) async-start(bf16[32,1024,64]{1,2,0:T(8,128)(2,1)} %stack.2), calls=%async_computation | async-start | bytes 8388608 | tf_op jit(solution)/shard_map/all_to_all | solution.py:97
  106.0 0.0 copy-start.7
  106.0 68.9 %all-reduce.2.cloned.1.call-done = bf16[768,2048]{1,0:T(8,128)(2,1)} async-done(((bf16[768,2048]{1,0:T(8,128)(2,1)}), bf16[768,2048]{1,0:T(8,128)(2,1)}) %all-reduce.2.cloned.1.call-update) | async-done | bytes 3145744 | tf_op jit(solution)/shard_map/psum | solution.py:85
  174.9 6.5 %convert_add_fusion = (f32[768,2048]{1,0:T(8,128)}, f32[768]{0:T(1024)S(1)}) fusion(bf16[768,2048]{1,0:T(8,128)(2,1)} %all-reduce.2.cloned.1.call-done, bf16[768,2048]{1,0:T(8,128)(2,1)} %all-gather.4.cloned.1.call-done), kind=kLoop, calls=%fused_computation.3 | loop fusion | flops 7863552 | bytes 12585984 | tf_op jit(solution)/shard_map/add | solution.py:86
  181.4 67.8 %all-gather.6.cloned.1.call-done = bf16[2048,2048]{1,0:T(8,128)(2,1)} async-done(((bf16[64,2048]{1,0:T(8,128)(2,1)}), bf16[2048,2048]{1,0:T(8,128)(2,1)}) %all-gather.6.cloned.1.call-update) | async-done | bytes 8388624 | tf_op jit(solution)/shard_map/all_gather | solution.py:36
  249.2 0.0 copy-done.7
  249.2 9.2 %fusion = f32[768,1024]{1,0:T(8,128)} fusion(bf16[2048,2048]{1,0:T(8,128)(2,1)} %all-gather.6.cloned.1.call-done, f32[2048]{0:T(1024)S(1)} %copy-done.7, f32[768]{0:T(1024)S(1)} %add_rsqrt_fusion.1, bf16[768,2048]{1,0:T(8,128)(2,1)} %all-reduce.2.cloned.1.call-done, bf16[768,2048]{1,0:T(8,128)(2,1)} %all-gather.4.cloned.1.call-done), kind=kOutput, calls=%fused_computation.5 | convolution fusion | flops 3230662656 | bytes 13642752 | tf_op jit(solution)/shard_map/dot_general | solution.py:92
  258.3 0.0 all-to-all-done
  258.3 14.8 %convolution_convert_fusion = bf16[768,2048]{1,0:T(8,128)(2,1)} fusion(bf16[1024,2048]{0,1:T(8,128)(2,1)} %bitcast.11, f32[768,1024]{1,0:T(8,128)} %fusion, bf16[2048,2048]{1,0:T(8,128)(2,1)} %all-gather.6.cloned.1.call-done, f32[2048]{0:T(1024)S(1)} %copy-done.7, f32[768]{0:T(1024)S(1)} %add_rsqrt_fusion.1, ...), kind=kOutput, calls=%fused_computation.9 | convolution fusion | flops 6458179584 | bytes 20982784 | tf_op jit(solution)/shard_map/dot_general | solution.py:94
  273.2 3.7 %copy.31 = bf16[96,8,8,256]{3,2,0,1:T(8,128)(2,1)} copy(bf16[96,8,8,256]{3,2,1,0:T(8,128)(2,1)} %bitcast.61) | data formatting | bytes 6291456 | tf_op jit(solution)/shard_map/reshape | solution.py:41
  276.9 4.8 %all-to-all-start.1 = ((bf16[8,768,256]{2,1,0:T(8,128)(2,1)}), bf16[8,768,256]{2,1,0:T(8,128)(2,1)}, u32[]{:S(2)}, u32[]{:S(2)}) async-start(bf16[8,768,256]{2,1,0:T(8,128)(2,1)} %bitcast.60), calls=%async_computation.1 | async-start | bytes 6291456 | tf_op jit(solution)/shard_map/all_to_all | solution.py:47
  281.7 37.6 %all-to-all-done.1 = bf16[8,768,256]{2,1,0:T(8,128)(2,1)} async-done(((bf16[8,768,256]{2,1,0:T(8,128)(2,1)}), bf16[8,768,256]{2,1,0:T(8,128)(2,1)}, u32[]{:S(2)}, u32[]{:S(2)}) %all-to-all-start.1) | async-done | bytes 3145760 | tf_op jit(solution)/shard_map/all_to_all | solution.py:47
  319.3 2.4 convert_reduce_fusion
  321.7 2.0 add_convert_fusion
  (2 shorter events, 0.0 us)
Async XLA Ops:
  7.4 83.3 %copy-start = (bf16[256,2048]{1,0:T(8,128)(2,1)S(1)}, bf16[256,2048]{1,0:T(8,128)(2,1)}, u32[]{:S(2)}) copy-start(bf16[256,2048]{1,0:T(8,128)(2,1)} %param.15) | copy-start | bytes 3145732
  7.4 40.5 %all-gather.4.cloned.1.call-start = ((), (), s32[]{:S(2)}) async-start(), calls=%async_computation.2 | async-start | bytes 3538944 | tf_op jit(solution)/shard_map/all_gather | solution.py:59
  8.1 166.8 %all-reduce.2.cloned.1.call-start = ((), (), s32[]{:S(2)}) async-start(), calls=%async_computation.3 | async-start | bytes 6291456 | tf_op jit(solution)/shard_map/psum | solution.py:85
  47.9 3.4 %copy-start.1 = (bf16[768,2048]{1,0:T(8,128)(2,1)S(1)}, bf16[768,2048]{1,0:T(8,128)(2,1)}, u32[]{:S(2)}) copy-start(bf16[768,2048]{1,0:T(8,128)(2,1)} %all-gather.4.cloned.1.call-done) | copy-start | bytes 9437188
  51.2 33.2 %copy-start.6 = (bf16[2048,256]{1,0:T(8,128)(2,1)S(1)}, bf16[2048,256]{1,0:T(8,128)(2,1)}, u32[]{:S(2)}) copy-start(bf16[2048,256]{1,0:T(8,128)(2,1)} %param.11) | copy-start | bytes 3145732
  85.6 0.7 copy-start.8
  87.6 2.9 copy-start.5
  93.4 0.9 copy-start.3
  93.4 1.0 copy-start.4
  93.4 1.7 copy-start.2
  93.4 155.8 %all-gather.6.cloned.1.call-start = ((), (), s32[]{:S(2)}) async-start(), calls=%async_computation.4 | async-start | bytes 8650752 | tf_op jit(solution)/shard_map/all_gather | solution.py:36
  97.7 160.7 %all-to-all-start = ((bf16[32,1024,64]{1,2,0:T(8,128)(2,1)}), bf16[32,1024,64]{1,2,0:T(8,128)(2,1)}, u32[]{:S(2)}, u32[]{:S(2)}) async-start(bf16[32,1024,64]{1,2,0:T(8,128)(2,1)} %stack.2), calls=%async_computation | async-start | bytes 8388608 | tf_op jit(solution)/shard_map/all_to_all | solution.py:97
  106.0 143.2 %copy-start.7 = (f32[2048]{0:T(1024)S(1)}, f32[2048]{0:T(1024)}, u32[]{:S(2)}) copy-start(f32[2048]{0:T(1024)} %param.16) | copy-start | bytes 24580
  276.9 42.4 %all-to-all-start.1 = ((bf16[8,768,256]{2,1,0:T(8,128)(2,1)}), bf16[8,768,256]{2,1,0:T(8,128)(2,1)}, u32[]{:S(2)}, u32[]{:S(2)}) async-start(bf16[8,768,256]{2,1,0:T(8,128)(2,1)} %bitcast.60), calls=%async_computation.1 | async-start | bytes 6291456 | tf_op jit(solution)/shard_map/all_to_all | solution.py:47
Sparse Core Ops, SparseCore 0:
  10.0 37.8 all-gather.3
  93.5 81.2 all-reduce.1
Sparse Core Ops, SparseCore 1:
  96.5 152.6 all-gather.5
